TPU v7x, 32 devices: a whole 2x2x4 slice. The times are simulated.
32 devices in a mesh: section: 4 (over y, core), expert: 2 (over x), tensor: 4 (over z).
Axes of the slice: x: 2, y: 2, z: 4, core: 2. Of those that a mesh axis runs over, the one named last changes fastest.
Arguments:
- branch_weights: bfloat16 [2, 8192, 8192], P('expert', ('section', 'tensor')), may hold values from -0.125 to 0.125
- branch_gains: float32 [2, 8192], P('expert', ('section', 'tensor')), may hold values from 0.1 to 1.9
- column_order: int32 [2, 8192], P('expert'), may hold values from 0 to 8191, each once within a row
- layer_order: int32 [4], replicated, may hold values from 0 to 3, each once
- probe_seeds: int32 [1024], replicated, may hold values from 1 to 32767
Outputs:
- expert_weights: bfloat16 [2, 8192, 8192], P('expert', None, ('section', 'tensor'))
- checksum: float32 [2, 1024, 8192], P('expert', None, ('section', 'tensor'))
- fingerprint: float32 [2, 1024], P('expert')
- shared_gain: float32 [8192], replicated
Inputs may be any that keep to these rules, and one draw needn't show every extreme that they name: Each row of column_order names every hidden unit once. layer_order names every layer once.
All inputs are finite; a program needn't handle non-finite values.
Results may differ from a plain program's by a relative error of at most 0.0034.
Values may be sent and summed in bfloat16 or wider, within the bound.
A program may use at most 64 MiB of HBM per device.

v0:
```python
import jax
import jax.numpy as jnp
from jax import lax
from jax.sharding import PartitionSpec as P

D = 2048
FF = 8192


def probe_at(probe_seeds, row_ids):
    hashed = probe_seeds[:, None] * (row_ids[None, :] + 1) % 65521
    return (hashed % 511 - 255).astype(jnp.float32) / 256.0


def sketch(natural, probe_seeds):
    segment_rows = D // 2
    running = jnp.zeros((probe_seeds.shape[0], natural.shape[1]), jnp.float32)
    for portion in range(natural.shape[0] // segment_rows):
        row_ids = portion * segment_rows + lax.iota(jnp.int32, segment_rows)
        probes = probe_at(probe_seeds, row_ids).astype(jnp.bfloat16)
        running = running + jnp.dot(
            probes,
            natural[portion * segment_rows : (portion + 1) * segment_rows],
            preferred_element_type=jnp.float32,
        )
    return running


def local(branch_weights, branch_gains, column_order, layer_order, probe_seeds):
    weights = branch_weights[0]
    rows_dev = weights.shape[0]
    n_section = lax.axis_size("section")
    n_tensor = lax.axis_size("tensor")
    groups = n_section * n_tensor
    cols_dev = weights.shape[1] // groups
    layers = layer_order.shape[0]
    own_gains = branch_gains[0]
    mean_gains = lax.psum(own_gains, "expert") / lax.axis_size("expert")
    scaling = own_gains / mean_gains
    permuted = jnp.take(weights, column_order[0], axis=1)
    folded = (permuted.astype(jnp.float32) * scaling[:, None]).astype(jnp.bfloat16)
    per_layer = D // rows_dev
    slot_ids = lax.iota(jnp.int32, layers)
    inverse = jnp.sum(
        jnp.where(layer_order[None, :] == slot_ids[:, None], slot_ids[None, :], 0), axis=1
    )
    block_ids = lax.iota(jnp.int32, groups)
    layer_ids = block_ids // per_layer
    source_pos = (
        jnp.sum(jnp.where(layer_ids[:, None] == slot_ids[None, :], inverse[None, :], 0), axis=1)
        * per_layer
        + block_ids % per_layer
    )
    all_gains = lax.all_gather(mean_gains, ("section", "tensor"), axis=0, tiled=True)
    shared_gain = all_gains.reshape(groups, rows_dev)[source_pos].reshape(groups * rows_dev)
    device = lax.axis_index(("section", "tensor"))
    seven = jnp.full((1,), 7919, jnp.int32)
    arrived = lax.all_to_all(
        folded.reshape(rows_dev, groups, cols_dev),
        ("section", "tensor"),
        split_axis=1,
        concat_axis=0,
        tiled=True,
    )
    width_cols = arrived.shape[2]
    ordered = arrived.reshape(groups, rows_dev, width_cols)[source_pos].reshape(
        groups * rows_dev, width_cols
    )
    sketches = sketch(ordered, probe_seeds)
    column_probe = probe_at(seven, device * cols_dev + lax.iota(jnp.int32, cols_dev))[0]
    partial_print = jnp.dot(sketches, column_probe, precision=lax.Precision.HIGHEST)
    fingerprint = lax.psum(partial_print, ("section", "tensor")) * FF ** (-0.5)
    return (ordered[None], sketches[None], fingerprint[None], shared_gain)


def solution(mesh):
    return jax.shard_map(
        local,
        mesh=mesh,
        in_specs=(
            P("expert", ("section", "tensor"), None),
            P("expert", ("section", "tensor")),
            P("expert", None),
            P(),
            P(),
        ),
        out_specs=(
            P("expert", None, ("section", "tensor")),
            P("expert", None, ("section", "tensor")),
            P("expert", None),
            P(),
        ),
        check_vma=False,
    )
```

profile of v0, /device:TPU:0, one launch (start us, length us, event | category | flops | bytes accessed | tf_op | source)
XLA Modules:
  0.0 384.2 jit_solution(6322284176018858667)
XLA Ops:
  0.6 6.0 %psum.14 = f32[512]{0:T(512)S(1)} all-reduce(f32[512]{0:T(512)} %bitcast.67), channel_id=1, replica_groups=mesh['section'=4,'expert'=2,'tensor'=4] {'expert'}, use_global_device_ids=true, to_apply=%region_0.0 | all-reduce | flops 512 | bytes 4096 | tf_op jit(solution)/shard_map/psum | solution.py:38
  6.6 0.7 broadcast_multiply_fusion.1
  7.3 0.0 copy-start.1
  7.3 11.9 %copy.16 = bf16[1,512,8192]{1,2,0:T(8,128)(2,1)} copy(bf16[1,512,8192]{2,1,0:T(8,128)(2,1)} %param.5) | data formatting | bytes 16777216 | tf_op args[0]
  19.3 0.0 copy-done.1
  19.3 38.2 %gather_fusion = bf16[8192,512]{1,0:T(8,128)(2,1)} fusion(bf16[512,8192]{0,1:T(8,128)(2,1)} %bitcast.48, s32[8192]{0:T(1024)S(1)} %broadcast_clamp_fusion), kind=kCustom, calls=%fused_computation | custom fusion | bytes 16809984 | tf_op jit(solution)/shard_map/jit(_take)/gather | solution.py:40
  57.6 12.3 %copy.17 = bf16[512,16,512]{2,0,1:T(8,128)(2,1)} copy(bf16[512,16,512]{0,2,1:T(8,128)(2,1)} %bitcast.49) | data formatting | bytes 16777216 | tf_op jit(solution)/shard_map/jit(_take)/gather | solution.py:40
  69.8 0.5 broadcast.368
  70.3 0.7 reduce.3
  71.1 9.0 %multiply_convert_fusion = bf16[512,16,512]{2,0,1:T(8,128)(2,1)} fusion(f32[512]{0:T(512)S(1)} %get-tuple-element.13, bf16[512,16,512]{2,0,1:T(8,128)(2,1)} %copy.17, pred[16,512]{1,0:T(8,128)(4,1)S(1)} %compare_and_fusion), kind=kLoop, calls=%fused_computation.3 | loop fusion | flops 16777216 | bytes 16787456 | tf_op jit(solution)/shard_map/convert_element_type | solution.py:41
  80.1 0.0 copy-start.3
  80.1 6.7 %all-to-all-start = ((bf16[512,16,512]{2,0,1:T(8,128)(2,1)}), bf16[512,16,512]{2,0,1:T(8,128)(2,1)}, u32[]{:S(2)}, u32[]{:S(2)}) async-start(bf16[512,16,512]{2,0,1:T(8,128)(2,1)} %multiply_convert_fusion), calls=%async_computation | async-start | bytes 16777216 | tf_op jit(solution)/shard_map/all_to_all | solution.py:58
  86.7 207.0 %all-gather = f32[16,1,512]{2,1,0:T(1,128)S(1)} all-gather(f32[1,1,512]{2,1,0:T(1,128)S(1)} %bitcast.66), channel_id=1, replica_groups=mesh['section'=4,'expert'=2,'tensor'=4] {'section','tensor'}, dimensions={0}, use_global_device_ids=true | all-gather | bytes 34816 | tf_op jit(solution)/shard_map/all_gather | solution.py:54
  293.7 0.0 copy-done.3
  293.7 0.1 select_reduce_fusion.1
  293.9 0.1 select_reduce_fusion
  294.0 0.6 gather_fusion.2
  294.5 0.6 copy.19
  295.3 0.0 all-to-all-done
  295.3 8.3 %gather_fusion.1 = bf16[16,512,512]{2,1,0:T(8,128)(2,1)} fusion(bf16[16,512,512]{2,1,0:T(8,128)(2,1)} %bitcast.8, s32[1024]{0:T(1024)S(1)} %pad_clamp_fusion), kind=kCustom, calls=%fused_computation.1 | custom fusion | bytes 16777280 | tf_op jit(solution)/shard_map/gather | solution.py:66
  303.6 0.0 copy-start.2
  303.6 4.4 %fusion.212 = (bf16[2,512,512]{2,1,0:T(8,128)(2,1)S(1)}, bf16[2,512,512]{2,1,0:T(8,128)(2,1)S(1)}, bf16[2,512,512]{2,1,0:T(8,128)(2,1)S(1)}, bf16[2,512,512]{2,1...) fusion(bf16[16,512,512]{2,1,0:T(8,128)(2,1)} %gather_fusion.1), kind=kLoop, calls=%fused_computation.260 | loop fusion | bytes 16777216 | tf_op jit(solution)/shard_map/slice | solution.py:23
  308.0 0.0 copy-done.2
  308.0 5.3 %fusion.100 = f32[1024,512]{1,0:T(8,128)S(1)} fusion(bf16[1024,512]{1,0:T(8,128)(2,1)S(1)} %bitcast.60, s32[1024]{0:T(1024)S(1)} %iota_add_fusion.6, s32[1024]{0:T(1024)S(1)} %copy-done.2), kind=kOutput, calls=%fused_computation.122 | convolution fusion | flops 1091567616 | bytes 3153920 | tf_op jit(solution)/shard_map/dot_general | solution.py:21
  313.3 5.3 %fusion.88 = f32[1024,512]{1,0:T(8,128)S(1)} fusion(bf16[1024,512]{1,0:T(8,128)(2,1)S(1)} %bitcast.59, s32[1024]{0:T(1024)S(1)} %iota_add_fusion, s32[1024]{0:T(1024)S(1)} %copy-done.2), kind=kOutput, calls=%fused_computation.116 | convolution fusion | flops 1091567616 | bytes 3153920 | tf_op jit(solution)/shard_map/dot_general | solution.py:21
  318.5 5.5 %fusion.90 = f32[1024,512]{1,0:T(8,128)S(1)} fusion(bf16[1024,512]{1,0:T(8,128)(2,1)S(1)} %bitcast.58, s32[1024]{0:T(1024)S(1)} %iota_add_fusion.1, s32[1024]{0:T(1024)S(1)} %copy-done.2), kind=kOutput, calls=%fused_computation.117 | convolution fusion | flops 1091567616 | bytes 3153920 | tf_op jit(solution)/shard_map/dot_general | solution.py:21
  324.0 5.3 %fusion.92 = f32[1024,512]{1,0:T(8,128)S(1)} fusion(bf16[1024,512]{1,0:T(8,128)(2,1)S(1)} %bitcast.57, s32[1024]{0:T(1024)S(1)} %iota_add_fusion.2, s32[1024]{0:T(1024)S(1)} %copy-done.2), kind=kOutput, calls=%fused_computation.118 | convolution fusion | flops 1091567616 | bytes 3153920 | tf_op jit(solution)/shard_map/dot_general | solution.py:21
  329.3 5.5 %fusion.94 = f32[1024,512]{1,0:T(8,128)S(1)} fusion(bf16[1024,512]{1,0:T(8,128)(2,1)S(1)} %bitcast.56, s32[1024]{0:T(1024)S(1)} %iota_add_fusion.3, s32[1024]{0:T(1024)S(1)} %copy-done.2), kind=kOutput, calls=%fused_computation.119 | convolution fusion | flops 1091567616 | bytes 3153920 | tf_op jit(solution)/shard_map/dot_general | solution.py:21
  334.8 5.3 %fusion.96 = f32[1024,512]{1,0:T(8,128)S(1)} fusion(bf16[1024,512]{1,0:T(8,128)(2,1)S(1)} %bitcast.55, s32[1024]{0:T(1024)S(1)} %iota_add_fusion.4, s32[1024]{0:T(1024)S(1)} %copy-done.2), kind=kOutput, calls=%fused_computation.120 | convolution fusion | flops 1091567616 | bytes 3153920 | tf_op jit(solution)/shard_map/dot_general | solution.py:21
  340.1 5.5 %fusion.98 = f32[1024,512]{1,0:T(8,128)S(1)} fusion(bf16[1024,512]{1,0:T(8,128)(2,1)S(1)} %bitcast.54, s32[1024]{0:T(1024)S(1)} %iota_add_fusion.5, s32[1024]{0:T(1024)S(1)} %copy-done.2), kind=kOutput, calls=%fused_computation.121 | convolution fusion | flops 1091567616 | bytes 3153920 | tf_op jit(solution)/shard_map/dot_general | solution.py:21
  345.6 6.0 %add_add_fusion = f32[1024,512]{1,0:T(8,128)S(1)} fusion(f32[1024,512]{1,0:T(8,128)S(1)} %fusion.88, f32[1024,512]{1,0:T(8,128)S(1)} %fusion.90, f32[1024,512]{1,0:T(8,128)S(1)} %fusion.92, f32[1024,512]{1,0:T(8,128)S(1)} %fusion.94, f32[1024,512]{1,0:T(8,128)S(1)} %fusion.96, f32[1024,512]{1,0:T(8,128)S(1)} %fusion.98, f32[1024,512]{1,0:T(8,128)S(1)} %fusion.100, ...), kind=kOutput, calls=%fused_computation.125 | convolution fusion | flops 1095237632 | bytes 17833984 | tf_op jit(solution)/shard_map/dot_general | solution.py:21
  351.6 0.0 copy-start
  351.6 1.9 fusion.213
  353.5 29.7 %psum.15 = f32[1024]{0:T(1024)S(1)} all-reduce(f32[1024]{0:T(1024)S(1)} %bitcast.64), channel_id=1, replica_groups=mesh['section'=4,'expert'=2,'tensor'=4] {'section','tensor'}, use_global_device_ids=true, to_apply=%region_3.4 | all-reduce | flops 1024 | bytes 8192 | tf_op jit(solution)/shard_map/psum | solution.py:72
  383.2 0.6 broadcast_multiply_fusion
  383.8 0.0 copy-done
  (17 shorter events, 0.1 us)
Async XLA Ops:
  7.3 11.9 %copy-start.1 = (s32[1,8192]{1,0:T(1,128)S(1)}, s32[1,8192]{1,0:T(1,128)}, u32[]{:S(2)}) copy-start(s32[1,8192]{1,0:T(1,128)} %param.7) | copy-start | bytes 98308
  80.1 213.7 %copy-start.3 = (s32[4]{0:T(128)S(1)}, s32[4]{0:T(128)}, u32[]{:S(2)}) copy-start(s32[4]{0:T(128)} %param.8) | copy-start | bytes 52
  80.1 215.2 %all-to-all-start = ((bf16[512,16,512]{2,0,1:T(8,128)(2,1)}), bf16[512,16,512]{2,0,1:T(8,128)(2,1)}, u32[]{:S(2)}, u32[]{:S(2)}) async-start(bf16[512,16,512]{2,0,1:T(8,128)(2,1)} %multiply_convert_fusion), calls=%async_computation | async-start | bytes 16777216 | tf_op jit(solution)/shard_map/all_to_all | solution.py:58
  303.6 4.4 %copy-start.2 = (s32[1024]{0:T(1024)S(1)}, s32[1024]{0:T(1024)}, u32[]{:S(2)}) copy-start(s32[1024]{0:T(1024)} %param.9) | copy-start | bytes 12292
  351.6 32.2 %copy-start = (f32[1024,512]{1,0:T(8,128)}, f32[1024,512]{1,0:T(8,128)S(1)}, u32[]{:S(2)}) copy-start(f32[1024,512]{1,0:T(8,128)S(1)} %add_add_fusion) | copy-start | bytes 6291460
where the time goes:
time: 390 us; the launch traced here: 384 us
  blocking collectives  243 us (62%)
  local copies, waits for them, and re-layouts  76.8 us (20%)
  matrix products  45.5 us (12%)
  other arithmetic  11.3 us (3%)
  starting transfers between devices  6.66 us (2%)
    all_gather x1, blocking collectives, local(): lax.all_gather(mean_gains, ('section', 'tensor'), axis=0, tiled=True)  207 us
    gather x2, local copies, waits for them, and re-layouts, local(): permuted = jnp.take(weights, column_order[0], axis=1)  50.5 us
    dot_general x8, matrix products, sketch(): jnp.dot(probes, natural[portion * segment_rows:(portion + 1) * segment_ro...  43.6 us
    psum x1, blocking collectives, local(): fingerprint = lax.psum(partial_print, ('section', 'tensor')) * FF ** (-0.5)  29.7 us
    unnamed x12, local copies, waits for them, and re-layouts  13.1 us
    convert_element_type x1, other arithmetic, local(): (permuted.astype(jnp.float32) * scaling[:, None]).astype(jnp.bfloat16)  8.97 us
    gather x1, local copies, waits for them, and re-layouts, local(): arrived.reshape(groups, rows_dev, width_cols)[source_pos]  8.32 us
  transfers between devices with their start and end apart: 1, of which 0 were waited for; matrix products, arithmetic and copies ran while one was open for 0% of the time, Pallas kernels for 0%

commit v1 on v0

v1 whole, which is shorter than its diff:
```python
import functools

import jax
import jax.numpy as jnp
from jax import lax
from jax.experimental import pallas as pl
from jax.experimental.pallas import tpu as pltpu
from jax.sharding import PartitionSpec as P

MESH = pl.DeviceIdType.MESH


def probe_values(products):
    folded = (products >> 16) * 15 + (products & 65535)
    hashed = jnp.where(folded >= 65521, folded - 65521, folded)
    digits = (hashed >> 9) + (hashed & 511)
    digits = jnp.where(digits >= 511, digits - 511, digits)
    return (digits - 255).astype(jnp.float32) * (1.0 / 256.0)


def exchange(
    n_section, n_expert, n_tensor, layers,
    order_s, w_hbm, gains_ref, cols_ref, seeds_ref,
    arrived_hbm, sums_ref, print_ref, means_ref,
    w, staged, arrived, acc, onehot, scale, print_acc, seed_col, probes, gains, parts,
    w_sem, send_sem, recv_sem, out_sem, gain_send, gain_recv, mean_send, mean_recv,
    part_send, part_recv,
):
    section, expert, tensor = (lax.axis_index(a) for a in ("section", "expert", "tensor"))
    groups = n_section * n_tensor
    me = section * n_tensor + tensor
    rows, width = w.shape
    cols = width // groups
    n_probes = seed_col.shape[0]
    deep = onehot.shape[0]
    n_deep = width // deep
    per_layer = groups // layers
    half = n_tensor // 2 if n_tensor % 2 == 0 else n_tensor
    sides = n_tensor // half

    def partner(k, sign):
        m, cross = k // sides, (k + 1) % sides
        j, i = (m + 1) % half, (m // half + 1) % n_section
        t = ((tensor // half + cross) % sides) * half + (tensor % half + sign * j + half) % half
        return (section + sign * i + n_section) % n_section, t

    def remote(src, dst, send, recv, k):
        s, t = partner(k, 1)
        return pltpu.make_async_remote_copy(
            src_ref=src, dst_ref=dst, send_sem=send.at[k], recv_sem=recv.at[k],
            device_id={"section": s, "tensor": t}, device_id_type=MESH)

    def block_copy(k):
        s, t = partner(k, 1)
        return remote(staged.at[s * n_tensor + t], arrived.at[me], send_sem, recv_sem, k)

    def mean_copy(k):
        return remote(means_ref.at[me], means_ref.at[me], mean_send, mean_recv, k)

    def part_copy(k):
        return remote(parts.at[me], parts.at[me], part_send, part_recv, k)

    def gain_copy(j):
        return pltpu.make_async_remote_copy(
            src_ref=gains_ref, dst_ref=gains.at[expert], send_sem=gain_send.at[j],
            recv_sem=gain_recv.at[j], device_id={"expert": (expert + j + 1) % n_expert},
            device_id_type=MESH)

    def w_copy(c):
        at = pl.ds(pl.multiple_of(c * deep, deep), deep)
        return pltpu.make_async_copy(w_hbm.at[0, :, at], w.at[:, at], w_sem.at[c])

    def out_copy(k, g):
        return pltpu.make_async_copy(arrived.at[g], arrived_hbm.at[g], out_sem.at[k])

    @pl.loop(0, n_deep)
    def _(c):
        w_copy(c).start()

    barrier = pltpu.get_barrier_semaphore()

    @pl.loop(0, groups - 1)
    def _(k):
        s, t = partner(k, 1)
        pl.semaphore_signal(
            barrier, inc=1, device_id={"section": s, "tensor": t}, device_id_type=MESH)

    @pl.loop(0, n_expert - 1)
    def _(j):
        pl.semaphore_signal(
            barrier, inc=1, device_id={"expert": (expert + j + 1) % n_expert},
            device_id_type=MESH)

    print_acc[...] = jnp.zeros_like(print_acc)
    sums_ref[...] = jnp.zeros_like(sums_ref)
    seeds = seeds_ref[...]
    seed_col[...] = jnp.broadcast_to(
        seeds.astype(jnp.float32), (128, n_probes)).T.astype(jnp.int32)
    pl.semaphore_wait(barrier, groups - 1 + n_expert - 1)

    @pl.loop(0, n_expert - 1)
    def _(j):
        gain_copy(j).start()

    own = gains_ref[...]
    gains[expert] = own

    @pl.loop(0, n_expert - 1)
    def _(j):
        gain_copy(j).wait()

    total = gains[0]
    for e in range(1, n_expert):
        total = total + gains[e]
    mean = total / n_expert
    means_ref[me] = mean
    scale[...] = jnp.broadcast_to(own / mean, (128, rows)).T

    @pl.loop(0, groups - 1)
    def _(k):
        mean_copy(k).start()

    @pl.loop(0, groups)
    def _(k):
        s, t = partner(k, 1)
        g = s * n_tensor + t
        at = pl.ds(pl.multiple_of(g * cols, cols), cols)
        wanted = cols_ref[:, at]
        acc[...] = jnp.zeros_like(acc)

        @pl.loop(0, n_deep)
        def _(c):
            @pl.when(k == 0)
            def _():
                w_copy(c).wait()

            ids = lax.broadcasted_iota(jnp.int32, (deep, cols), 0)
            onehot[...] = jnp.where(ids == wanted - c * deep, 1.0, 0.0).astype(jnp.bfloat16)
            acc[...] += jnp.dot(
                w[:, pl.ds(pl.multiple_of(c * deep, deep), deep)], onehot[...],
                preferred_element_type=jnp.float32)

        column_ids = g * cols + lax.broadcasted_iota(jnp.int32, (1, cols), 1)
        column_probe = probe_values(7919 * (column_ids + 1))
        for c in range(cols // 128):
            part = slice(c * 128, (c + 1) * 128)
            block = (acc[:, part] * scale[...]).astype(jnp.bfloat16)
            staged[g, :, part] = block
            print_acc[...] += block.astype(jnp.float32) * column_probe[:, part]

        @pl.when(k < groups - 1)
        def _():
            block_copy(k).start()

    def first_row(g):
        return order_s[g // per_layer] * (rows * per_layer) + (g % per_layer) * rows

    totals = jnp.sum(print_acc[...], axis=1, keepdims=True)
    row_ids = first_row(me) + lax.broadcasted_iota(jnp.int32, (rows, 128), 0)
    for c in range(n_probes // 128):
        part = slice(c * 128, (c + 1) * 128)
        values = probe_values(seeds[:, part] * (row_ids + 1))
        parts[me, :, part] = jnp.sum(values * totals, axis=0, keepdims=True)

    @pl.loop(0, groups - 1)
    def _(k):
        part_copy(k).start()

    def sketch(k, block):
        s, t = partner(k, -1)
        g = s * n_tensor + t
        first = first_row(g) + 1
        chunk = min(64, n_probes)

        @pl.loop(0, n_probes // chunk)
        def _(r):
            at = pl.ds(pl.multiple_of(r * chunk, chunk), chunk)
            for c in range(rows // 128):
                ids = first + c * 128 + lax.broadcasted_iota(jnp.int32, (1, 128), 1)
                probes[at, c * 128:(c + 1) * 128] = probe_values(
                    seed_col[at, :] * ids).astype(jnp.bfloat16)

        sums_ref[...] += jnp.dot(probes[...], block, preferred_element_type=jnp.float32)

    arrived[me] = staged[me]
    out_copy(groups - 1, me).start()
    sketch(groups - 1, staged[me])

    @pl.loop(0, groups - 1)
    def _(k):
        s, t = partner(k, -1)
        g = s * n_tensor + t
        block_copy(k).wait_recv()
        out_copy(k, g).start()
        sketch(k, arrived[g])

    @pl.loop(0, groups - 1)
    def _(k):
        part_copy(k).wait()
        mean_copy(k).wait()

    printed = parts[0]
    for g in range(1, groups):
        printed = printed + parts[g]
    print_ref[...] = printed * width ** -0.5

    @pl.loop(0, groups - 1)
    def _(k):
        s, t = partner(k, -1)
        block_copy(k).wait_send()
        out_copy(k, s * n_tensor + t).wait()

    out_copy(groups - 1, me).wait()


def place(order_s, blocks_ref, sums_ref, print_ref, means_ref,
          weights_out, sums_out, print_out, means_out):
    weights_out[...] = blocks_ref[...]
    sums_out[...] = sums_ref[...]
    print_out[...] = print_ref[...]
    means_out[...] = means_ref[...]


def local(n_section, n_expert, n_tensor, branch_weights, branch_gains, column_order,
          layer_order, probe_seeds):
    _, rows, width = branch_weights.shape
    groups = n_section * n_tensor
    cols = width // groups
    layers = layer_order.shape[0]
    n_probes = probe_seeds.shape[0]
    per_layer = groups // layers
    deep = min(1024, width)
    f32, bf16 = jnp.float32, jnp.bfloat16
    vmem = pl.BlockSpec(memory_space=pltpu.VMEM)
    hbm = pl.BlockSpec(memory_space=pl.ANY)
    dma = pltpu.SemaphoreType.DMA
    arrived, sums, printed, means = pl.pallas_call(
        functools.partial(exchange, n_section, n_expert, n_tensor, layers),
        out_shape=(
            jax.ShapeDtypeStruct((groups, rows, cols), bf16),
            jax.ShapeDtypeStruct((n_probes, cols), f32),
            jax.ShapeDtypeStruct((1, n_probes), f32),
            jax.ShapeDtypeStruct((groups, 1, rows), f32),
        ),
        in_specs=[pl.BlockSpec(memory_space=pltpu.SMEM), hbm, vmem, vmem, vmem],
        out_specs=(hbm, vmem, vmem, vmem),
        scratch_shapes=[
            pltpu.VMEM((rows, width), bf16),
            pltpu.VMEM((groups, rows, cols), bf16),
            pltpu.VMEM((groups, rows, cols), bf16),
            pltpu.VMEM((rows, cols), f32),
            pltpu.VMEM((deep, cols), bf16),
            pltpu.VMEM((rows, 128), f32),
            pltpu.VMEM((rows, 128), f32),
            pltpu.VMEM((n_probes, 128), jnp.int32),
            pltpu.VMEM((n_probes, rows), bf16),
            pltpu.VMEM((n_expert, 1, rows), f32),
            pltpu.VMEM((groups, 1, n_probes), f32),
            dma((width // deep,)), dma((groups,)), dma((groups,)), dma((groups,)),
            dma((n_expert,)), dma((n_expert,)), dma((groups,)), dma((groups,)),
            dma((groups,)), dma((groups,)),
        ],
        compiler_params=pltpu.CompilerParams(
            collective_id=0, has_side_effects=True, vmem_limit_bytes=56 * 2 ** 20),
        name="exchange",
    )(layer_order, branch_weights, branch_gains, column_order, probe_seeds.reshape(1, n_probes))

    def placed(g, order):
        return (order[g // per_layer] * per_layer + g % per_layer, 0, 0)

    share = n_probes // groups
    weights, sums, printed, means = pl.pallas_call(
        place,
        grid_spec=pltpu.PrefetchScalarGridSpec(
            num_scalar_prefetch=1,
            grid=(groups,),
            in_specs=[
                pl.BlockSpec((1, rows, cols), lambda g, order: (g, 0, 0)),
                pl.BlockSpec((share, cols), lambda g, order: (g, 0)),
                pl.BlockSpec((1, n_probes), lambda g, order: (0, 0)),
                pl.BlockSpec((1, 1, rows), lambda g, order: (g, 0, 0)),
            ],
            out_specs=[
                pl.BlockSpec((1, rows, cols), placed),
                pl.BlockSpec((share, cols), lambda g, order: (g, 0)),
                pl.BlockSpec((1, n_probes), lambda g, order: (0, 0)),
                pl.BlockSpec((1, 1, rows), placed),
            ],
        ),
        out_shape=(
            jax.ShapeDtypeStruct((groups, rows, cols), bf16),
            jax.ShapeDtypeStruct((n_probes, cols), f32),
            jax.ShapeDtypeStruct((1, n_probes), f32),
            jax.ShapeDtypeStruct((groups, 1, rows), f32),
        ),
        name="place",
    )(layer_order, arrived, sums, printed, means)
    return (weights.reshape(1, groups * rows, cols), sums[None], printed,
            means.reshape(groups * rows))


def solution(mesh):
    sizes = mesh.shape
    return jax.shard_map(
        functools.partial(local, sizes["section"], sizes["expert"], sizes["tensor"]),
        mesh=mesh,
        in_specs=(
            P("expert", ("section", "tensor"), None),
            P("expert", ("section", "tensor")),
            P("expert", None),
            P(),
            P(),
        ),
        out_specs=(
            P("expert", None, ("section", "tensor")),
            P("expert", None, ("section", "tensor")),
            P("expert", None),
            P(),
        ),
        check_vma=False,
    )
```

time: 390 us -> 223 us (0.57); the launches traced: 384 us -> 223 us
  blocking collectives: 243 us -> 0 us
  Pallas kernels: 0 us -> 222 us
  local copies, waits for them, and re-layouts: 76.8 us -> 0 us
  matrix products: 45.5 us -> 0 us
  other arithmetic: 11.3 us -> 0 us
  starting transfers between devices: 6.66 us -> 0 us
    pallas_call x0 -> x2, Pallas kernels: none -> 222 us  [the longest x1 208 us: local(): pl.pallas_call(functools.partial(exchange, n_section, n_expert, n_tensor,...]
    all_gather x1 -> x0, blocking collectives: 207 us -> none  [local(): lax.all_gather(mean_gains, ('section', 'tensor'), axis=0, tiled=True)]
    gather x4 -> x0, local copies, waits for them, and re-layouts: 59.4 us -> none  [the longest x2 50.5 us: local(): permuted = jnp.take(weights, column_order[0], axis=1)]
    dot_general x9 -> x0, matrix products: 45.5 us -> none  [the longest x8 43.6 us: sketch(): jnp.dot(probes, natural[portion * segment_rows:(portion + 1) * segment_ro...]
    psum x2 -> x0, blocking collectives: 35.7 us -> none  [the longest x1 29.7 us: local(): fingerprint = lax.psum(partial_print, ('section', 'tensor')) * FF ** (-0.5)]
    unnamed x12 -> x0, local copies, waits for them, and re-layouts: 13.1 us -> none
    convert_element_type x1 -> x0, other arithmetic: 8.97 us -> none  [local(): (permuted.astype(jnp.float32) * scaling[:, None]).astype(jnp.bfloat16)]
    all_to_all x1 -> x0, starting transfers between devices: 6.66 us -> none  [local(): lax.all_to_all(folded.reshape(rows_dev, groups, cols_dev), ('section', 't...]
  transfers between devices with their start and end apart: 1 -> 0, of which waited for: 0 -> 0; matrix products, arithmetic and copies ran while one was open for 0% -> 0% of each run, Pallas kernels for 0% -> 0%
where the time goes in v1:
time: 223 us
  Pallas kernels  222 us (100%)
    pallas_call x1, Pallas kernels, local(): pl.pallas_call(functools.partial(exchange, n_section, n_expert, n_tensor,...  208 us
    pallas_call x1, Pallas kernels, local(): pl.pallas_call(place, grid_spec=pltpu.PrefetchScalarGridSpec(num_scalar_p...  13.7 us

profile of v1, /device:TPU:0, one launch (start us, length us, event | category | flops | bytes accessed | tf_op | source)
XLA Modules:
  0.0 222.5 jit_solution(2757934602497279784)
XLA Ops:
  0.6 208.1 %exchange.1 = (bf16[16,512,512]{2,1,0:T(8,128)(2,1)}, f32[1024,512]{1,0:T(8,128)}, f32[1,1024]{1,0:T(1,128)}, f32[16,1,512]{2,1,0:T(1,128)}) custom-call(s32[4]{0:T(128)} %order_s.3, bf16[1,512,8192]{2,1,0:T(8,128)(2,1)} %w_hbm.1, f32[1,512]{1,0:T(1,128)} %gains_ref.1, s32[1,8192]{1,0:T(1,128)} %cols_ref.1, s32[1,1024]{1,0:T(1,128)} %bitcast.4), custom_call_target="tpu_custom_call" | custom-call | tf_op jit(solution)/shard_map/exchange/pallas_call | solution.py:237
  208.8 13.7 %place.1 = (bf16[16,512,512]{2,1,0:T(8,128)(2,1)}, f32[1024,512]{1,0:T(8,128)}, f32[1,1024]{1,0:T(1,128)}, f32[16,1,512]{2,1,0:T(1,128)}) custom-call(s32[4]{0:T(128)} %order_s.3, bf16[16,512,512]{2,1,0:T(8,128)(2,1)} %get-tuple-element.12.blocks_ref, f32[1024,512]{1,0:T(8,128)} %get-tuple-element.13.sums_ref, f32[1,1024]{1,0:T(1,128)} %get-tuple-element.14.print_ref, ...), custom_call_target="tpu_custom_call" | custom-call | tf_op jit(solution)/shard_map/place/pallas_call | solution.py:272

commit v2 on v1

--- a/solution.py
+++ b/solution.py
@@ -21,9 +21,9 @@
 def exchange(
     n_section, n_expert, n_tensor, layers,
     order_s, w_hbm, gains_ref, cols_ref, seeds_ref,
-    arrived_hbm, sums_ref, print_ref, means_ref,
-    w, staged, arrived, acc, onehot, scale, print_acc, seed_col, probes, gains, parts,
-    w_sem, send_sem, recv_sem, out_sem, gain_send, gain_recv, mean_send, mean_recv,
+    arrived, sums_ref, print_ref, means_ref,
+    w, staged, acc, onehot, scale, print_acc, seed_col, probes, gains, parts,
+    w_sem, send_sem, recv_sem, gain_send, gain_recv, mean_send, mean_recv,
     part_send, part_recv,
 ):
     section, expert, tensor = (lax.axis_index(a) for a in ("section", "expert", "tensor"))
@@ -40,7 +40,9 @@
 
     def partner(k, sign):
         m, cross = k // sides, (k + 1) % sides
-        j, i = (m + 1) % half, (m // half + 1) % n_section
+        j = cross * (m // n_section % half) + (1 - cross) * ((m + 1) % half)
+        q = cross * (m % n_section) + (1 - cross) * ((m + 1) // half % n_section)
+        i = q if n_section % 2 else q % 2 * (n_section // 2) + q // 2
         t = ((tensor // half + cross) % sides) * half + (tensor % half + sign * j + half) % half
         return (section + sign * i + n_section) % n_section, t
 
@@ -70,9 +72,6 @@
         at = pl.ds(pl.multiple_of(c * deep, deep), deep)
         return pltpu.make_async_copy(w_hbm.at[0, :, at], w.at[:, at], w_sem.at[c])
 
-    def out_copy(k, g):
-        return pltpu.make_async_copy(arrived.at[g], arrived_hbm.at[g], out_sem.at[k])
-
     @pl.loop(0, n_deep)
     def _(c):
         w_copy(c).start()
@@ -92,33 +91,11 @@
             device_id_type=MESH)
 
     print_acc[...] = jnp.zeros_like(print_acc)
-    sums_ref[...] = jnp.zeros_like(sums_ref)
-    seeds = seeds_ref[...]
-    seed_col[...] = jnp.broadcast_to(
-        seeds.astype(jnp.float32), (128, n_probes)).T.astype(jnp.int32)
     pl.semaphore_wait(barrier, groups - 1 + n_expert - 1)
 
     @pl.loop(0, n_expert - 1)
     def _(j):
         gain_copy(j).start()
-
-    own = gains_ref[...]
-    gains[expert] = own
-
-    @pl.loop(0, n_expert - 1)
-    def _(j):
-        gain_copy(j).wait()
-
-    total = gains[0]
-    for e in range(1, n_expert):
-        total = total + gains[e]
-    mean = total / n_expert
-    means_ref[me] = mean
-    scale[...] = jnp.broadcast_to(own / mean, (128, rows)).T
-
-    @pl.loop(0, groups - 1)
-    def _(k):
-        mean_copy(k).start()
 
     @pl.loop(0, groups)
     def _(k):
@@ -139,6 +116,22 @@
             acc[...] += jnp.dot(
                 w[:, pl.ds(pl.multiple_of(c * deep, deep), deep)], onehot[...],
                 preferred_element_type=jnp.float32)
+
+        @pl.when(k == 0)
+        def _():
+            own = gains_ref[...]
+            gains[expert] = own
+
+            @pl.loop(0, n_expert - 1)
+            def _(j):
+                gain_copy(j).wait()
+
+            total = gains[0]
+            for e in range(1, n_expert):
+                total = total + gains[e]
+            mean = total / n_expert
+            means_ref[me] = mean
+            scale[...] = jnp.broadcast_to(own / mean, (128, rows)).T
 
         column_ids = g * cols + lax.broadcasted_iota(jnp.int32, (1, cols), 1)
         column_probe = probe_values(7919 * (column_ids + 1))
@@ -152,6 +145,15 @@
         def _():
             block_copy(k).start()
 
+    @pl.loop(0, groups - 1)
+    def _(k):
+        mean_copy(k).start()
+
+    sums_ref[...] = jnp.zeros_like(sums_ref)
+    seeds = seeds_ref[...]
+    seed_col[...] = jnp.broadcast_to(
+        seeds.astype(jnp.float32), (128, n_probes)).T.astype(jnp.int32)
+
     def first_row(g):
         return order_s[g // per_layer] * (rows * per_layer) + (g % per_layer) * rows
 
@@ -183,7 +185,6 @@
         sums_ref[...] += jnp.dot(probes[...], block, preferred_element_type=jnp.float32)
 
     arrived[me] = staged[me]
-    out_copy(groups - 1, me).start()
     sketch(groups - 1, staged[me])
 
     @pl.loop(0, groups - 1)
@@ -191,7 +192,6 @@
         s, t = partner(k, -1)
         g = s * n_tensor + t
         block_copy(k).wait_recv()
-        out_copy(k, g).start()
         sketch(k, arrived[g])
 
     @pl.loop(0, groups - 1)
@@ -206,19 +206,37 @@
 
     @pl.loop(0, groups - 1)
     def _(k):
-        s, t = partner(k, -1)
         block_copy(k).wait_send()
-        out_copy(k, s * n_tensor + t).wait()
-
-    out_copy(groups - 1, me).wait()
 
 
 def place(order_s, blocks_ref, sums_ref, print_ref, means_ref,
-          weights_out, sums_out, print_out, means_out):
-    weights_out[...] = blocks_ref[...]
-    sums_out[...] = sums_ref[...]
-    print_out[...] = print_ref[...]
-    means_out[...] = means_ref[...]
+          weights_out, sums_out, print_out, means_out, block_sem, mean_sem, flat_sem):
+    groups = blocks_ref.shape[0]
+    per_layer = groups // order_s.shape[0]
+
+    def copies(g):
+        to = order_s[g // per_layer] * per_layer + g % per_layer
+        return (pltpu.make_async_copy(blocks_ref.at[g], weights_out.at[to], block_sem.at[g]),
+                pltpu.make_async_copy(means_ref.at[g], means_out.at[to], mean_sem.at[g]))
+
+    flat = (pltpu.make_async_copy(sums_ref, sums_out, flat_sem.at[0]),
+            pltpu.make_async_copy(print_ref, print_out, flat_sem.at[1]))
+
+    @pl.loop(0, groups)
+    def _(g):
+        for copy in copies(g):
+            copy.start()
+
+    for copy in flat:
+        copy.start()
+
+    @pl.loop(0, groups)
+    def _(g):
+        for copy in copies(g):
+            copy.wait()
+
+    for copy in flat:
+        copy.wait()
 
 
 def local(n_section, n_expert, n_tensor, branch_weights, branch_gains, column_order,
@@ -243,10 +261,9 @@
             jax.ShapeDtypeStruct((groups, 1, rows), f32),
         ),
         in_specs=[pl.BlockSpec(memory_space=pltpu.SMEM), hbm, vmem, vmem, vmem],
-        out_specs=(hbm, vmem, vmem, vmem),
+        out_specs=(vmem, vmem, vmem, vmem),
         scratch_shapes=[
             pltpu.VMEM((rows, width), bf16),
-            pltpu.VMEM((groups, rows, cols), bf16),
             pltpu.VMEM((groups, rows, cols), bf16),
             pltpu.VMEM((rows, cols), f32),
             pltpu.VMEM((deep, cols), bf16),
@@ -256,43 +273,28 @@
             pltpu.VMEM((n_probes, rows), bf16),
             pltpu.VMEM((n_expert, 1, rows), f32),
             pltpu.VMEM((groups, 1, n_probes), f32),
-            dma((width // deep,)), dma((groups,)), dma((groups,)), dma((groups,)),
+            dma((width // deep,)), dma((groups,)), dma((groups,)),
             dma((n_expert,)), dma((n_expert,)), dma((groups,)), dma((groups,)),
             dma((groups,)), dma((groups,)),
         ],
         compiler_params=pltpu.CompilerParams(
-            collective_id=0, has_side_effects=True, vmem_limit_bytes=56 * 2 ** 20),
+            collective_id=0, has_side_effects=True, vmem_limit_bytes=40 * 2 ** 20),
         name="exchange",
     )(layer_order, branch_weights, branch_gains, column_order, probe_seeds.reshape(1, n_probes))
 
-    def placed(g, order):
-        return (order[g // per_layer] * per_layer + g % per_layer, 0, 0)
-
-    share = n_probes // groups
     weights, sums, printed, means = pl.pallas_call(
         place,
-        grid_spec=pltpu.PrefetchScalarGridSpec(
-            num_scalar_prefetch=1,
-            grid=(groups,),
-            in_specs=[
-                pl.BlockSpec((1, rows, cols), lambda g, order: (g, 0, 0)),
-                pl.BlockSpec((share, cols), lambda g, order: (g, 0)),
-                pl.BlockSpec((1, n_probes), lambda g, order: (0, 0)),
-                pl.BlockSpec((1, 1, rows), lambda g, order: (g, 0, 0)),
-            ],
-            out_specs=[
-                pl.BlockSpec((1, rows, cols), placed),
-                pl.BlockSpec((share, cols), lambda g, order: (g, 0)),
-                pl.BlockSpec((1, n_probes), lambda g, order: (0, 0)),
-                pl.BlockSpec((1, 1, rows), placed),
-            ],
-        ),
+        in_specs=[pl.BlockSpec(memory_space=pltpu.SMEM), vmem, vmem, vmem, vmem],
+        out_specs=(hbm, hbm, hbm, hbm),
+        scratch_shapes=[dma((groups,)), dma((groups,)), dma((2,))],
         out_shape=(
             jax.ShapeDtypeStruct((groups, rows, cols), bf16),
             jax.ShapeDtypeStruct((n_probes, cols), f32),
             jax.ShapeDtypeStruct((1, n_probes), f32),
             jax.ShapeDtypeStruct((groups, 1, rows), f32),
         ),
+        compiler_params=pltpu.CompilerParams(
+            has_side_effects=True, vmem_limit_bytes=16 * 2 ** 20),
         name="place",
     )(layer_order, arrived, sums, printed, means)
     return (weights.reshape(1, groups * rows, cols), sums[None], printed,

time: 223 us -> 207 us (0.928)
  Pallas kernels: 222 us -> 203 us
  local copies, waits for them, and re-layouts: 0 us -> 2.77 us
    pallas_call x1, Pallas kernels: 208 us -> 198 us  [local(): pl.pallas_call(functools.partial(exchange, n_section, n_expert, n_tensor,...]
    pallas_call x1, Pallas kernels: 13.7 us -> 4.87 us  [local(): pl.pallas_call(place, in_specs=[pl.BlockSpec(memory_space=pltpu.SMEM), vm...]
    unnamed x0 -> x8, local copies, waits for them, and re-layouts: none -> 2.77 us
where the time goes in v2:
time: 207 us
  Pallas kernels  203 us (98%)
  local copies, waits for them, and re-layouts  2.77 us (1%)
    pallas_call x1, Pallas kernels, local(): pl.pallas_call(functools.partial(exchange, n_section, n_expert, n_tensor,...  198 us
    pallas_call x1, Pallas kernels, local(): pl.pallas_call(place, in_specs=[pl.BlockSpec(memory_space=pltpu.SMEM), vm...  4.87 us

profile of v2, /device:TPU:0, one launch (start us, length us, event | category | flops | bytes accessed | tf_op | source)
XLA Modules:
  0.0 206.5 jit_solution(8092373129259360762)
XLA Ops:
  0.6 0.0 copy-start
  0.6 0.7 copy-done
  1.4 0.0 copy-start.1
  1.4 0.7 copy-done.1
  2.1 0.0 copy-start.2
  2.1 0.7 copy-done.2
  2.8 0.0 copy-start.3
  2.8 0.7 copy-done.3
  3.4 198.2 %exchange.1 = (bf16[16,512,512]{2,1,0:T(8,128)(2,1)S(1)}, f32[1024,512]{1,0:T(8,128)S(1)}, f32[1,1024]{1,0:T(1,128)S(1)}, f32[16,1,512]{2,1,0:T(1,128)S(1)}) custom-call(s32[4]{0:T(128)S(1)} %copy-done.3, bf16[1,512,8192]{2,1,0:T(8,128)(2,1)} %w_hbm.1, f32[1,512]{1,0:T(1,128)S(1)} %copy-done.2, s32[1,8192]{1,0:T(1,128)S(1)} %copy-done, s32[1,1024]{1,0:T(1,128)S(1)} %bitcast.4), custom_call_target="tpu_custom_call" | custom-call | tf_op jit(solution)/shard_map/exchange/pallas_call | solution.py:255
  201.6 4.9 %place.1 = (bf16[16,512,512]{2,1,0:T(8,128)(2,1)}, f32[1024,512]{1,0:T(8,128)}, f32[1,1024]{1,0:T(1,128)}, f32[16,1,512]{2,1,0:T(1,128)}) custom-call(s32[4]{0:T(128)S(1)} %copy-done.3, bf16[16,512,512]{2,1,0:T(8,128)(2,1)S(1)} %get-tuple-element.12.blocks_ref, f32[1024,512]{1,0:T(8,128)S(1)} %get-tuple-element.13.sums_ref, ...), custom_call_target="tpu_custom_call" | custom-call | tf_op jit(solution)/shard_map/place/pallas_call | solution.py:285
Async XLA Ops:
  0.6 0.8 copy-start
  1.4 0.7 copy-start.1
  2.1 0.7 copy-start.2
  2.8 0.7 copy-start.3
